TPU v7x, 128 devices: a whole 4x4x4 slice. The times are simulated.
128 devices in a mesh: stage: 1, model: 64 (over z, y, x), data: 2 (over core).
Axes of the slice: x: 4, y: 4, z: 4, core: 2. Of those that a mesh axis runs over, the one named last changes fastest.
Arguments:
- w_fc1: float32 [4, 1024, 1024], P('stage', 'data', 'model')
- m_fc1: float32 [4, 1024, 1024], P('stage', 'data', 'model')
- g_fc1: bfloat16 [4, 1024, 1024], P('stage', 'data', 'model')
- w_fc2: float32 [4, 1024, 512], P('stage', 'data', 'model')
- m_fc2: float32 [4, 1024, 512], P('stage', 'data', 'model')
- g_fc2: bfloat16 [4, 1024, 512], P('stage', 'data', 'model')
Outputs:
- output 1: float32 [4, 1024, 1024], P('stage', 'data', 'model')
- output 2: float32 [4, 1024, 1024], P('stage', 'data', 'model')
- output 3: float32 [4, 1024, 512], P('stage', 'data', 'model')
- output 4: float32 [4, 1024, 512], P('stage', 'data', 'model')
All inputs are finite; a program needn't handle non-finite values.
Results may differ from a plain program's by a relative error of at most 0.00735249.
Values are sent between devices in bfloat16 or wider.
A program may use at most 1 GiB of HBM per device.

v0:
```python
import math
import jax
import jax.numpy as jnp
from jax import lax
from jax.experimental import pallas as pl
from jax.experimental.pallas import tpu as pltpu
from jax.sharding import PartitionSpec as P

NS_STEPS = 5
NS_COEF_A = 3.4445
NS_COEF_B = -4.7750
NS_COEF_C = 2.0315
MOMENTUM = 0.95
LEARN_RATE = 0.04
DECAY = 0.2
NORM_EPS = 1e-7
F32 = jnp.float32
BF16 = jnp.bfloat16
RING = 4
EXPERTS = 4
ROWS = 512
C1, C2 = 16, 8
N1, N2 = 1024, 512
STEP_SCALE = 0.2 * math.sqrt(1024)
CHUNKS = (256, 256, 256, 256)
NORM_Z, DATA_Z1, DATA_Z2, NORM_P, DATA_P, OUT1, OUT2, SWAP = 0, 8, 12, 16, 32, 48, 52, 56
SEMS = 160


def dot(lhs, rhs, lhs_dim, rhs_dim):
    return lax.dot_general(lhs, rhs, (((lhs_dim,), (rhs_dim,)), ((), ())), preferred_element_type=F32)


def fold(sq):
    total = None
    for row in range(0, sq.shape[0], 8):
        for col in range(0, sq.shape[1], 128):
            tile = sq[row:row + 8, col:col + 128]
            total = tile if total is None else total + tile
    return total


def flip(pos, k):
    if k == 0:
        return pos
    if k == 1:
        return pos + 1 - 2 * lax.rem(pos, 2)
    if k == 2:
        return lax.rem(pos + 2, RING)
    return RING - 1 - pos


def kernel(m1h, g1h, m2h, g2h, o1, o2,
           m1, g1, m2, g2, mb1, mb2, nb, nz, npl, sx, gat1, gat2,
           ya, yb, aa, ab, ra, rb, b1, half, y2a, y2b, a2, b2, xo1, xo2, load_sem, send_sem, recv_sem):
    idx = lax.axis_index('model')
    core = lax.axis_index('data')
    z = lax.div(idx, 16)
    y = lax.rem(lax.div(idx, 4), 4)
    x = lax.rem(idx, 4)
    mesh_id = pl.DeviceIdType.MESH

    def at(dz, dy, dx, dc):
        return {'model': flip(z, dz) * 16 + flip(y, dy) * 4 + flip(x, dx), 'data': core if dc == 0 else 1 - core}

    partner = at(0, 0, 0, 1)
    count = [0]
    swaps = [0]
    sent = []

    def put(src, dst, target, slot):
        num = count[0]
        count[0] += 1
        copy = pltpu.make_async_remote_copy(
            src_ref=src, dst_ref=dst, send_sem=send_sem.at[num], recv_sem=recv_sem.at[slot],
            device_id=target, device_id_type=mesh_id)
        copy.start()
        sent.append(copy)
        return copy

    def trade(src, dst):
        swaps[0] += 1
        return put(src, dst, partner, SWAP + swaps[0] - 1)

    def arrived(dst, slot):
        pltpu.make_async_remote_copy(
            src_ref=dst, dst_ref=dst, send_sem=send_sem.at[0], recv_sem=recv_sem.at[slot],
            device_id=partner, device_id_type=mesh_id).wait_recv()

    def flush():
        while sent:
            sent.pop(0).wait_send()

    z_peers = [(dz, dc) for dz in range(RING) for dc in range(2) if (dz, dc) != (0, 0)]
    plane = [(dy, dx) for dy in range(RING) for dx in range(RING) if (dy, dx) != (0, 0)]
    greet = [at(dz, 0, 0, dc) for dz, dc in z_peers] + [at(0, dy, dx, 0) for dy, dx in plane]
    greet += [at(dz, 0, 1, 0) for dz in range(1, RING)]
    barrier = pltpu.get_barrier_semaphore()
    for target in greet:
        pl.semaphore_signal(barrier, inc=1, device_id=target, device_id_type=mesh_id)

    loads = [pltpu.make_async_copy(src, dst, load_sem.at[i])
             for i, (src, dst) in enumerate(((m1h, m1), (g1h, g1), (m2h, m2), (g2h, g2)))]
    for copy in loads:
        copy.start()
    for copy in loads:
        copy.wait()
    for e in range(EXPERTS):
        mom = MOMENTUM * m1[e] + g1[e].astype(F32)
        mb1[e] = mom.astype(BF16)
        nb[e, 0] = fold(mom * mom)
        mom = MOMENTUM * m2[e] + g2[e].astype(F32)
        mb2[e] = mom.astype(BF16)
        nb[e, 1] = fold(mom * mom)
    pl.semaphore_wait(barrier, len(greet))

    for dz, dc in z_peers:
        put(nb.at[flip(z, dz)], nz.at[dc, dz], at(dz, 0, 0, dc), NORM_Z + 4 * dc + dz)
    for k in range(1, RING):
        put(mb1.at[flip(z, k)], gat1.at[0, k], at(k, 0, 0, 0), DATA_Z1 + k)
    for k in range(1, RING):
        put(mb2.at[flip(z, k)], gat2.at[0, k], at(k, 0, 0, 0), DATA_Z2 + k)
    gat1[0, 0] = mb1[z]
    gat2[0, 0] = mb2[z]
    part = nb[z]
    for dz, dc in z_peers:
        arrived(nz.at[dc, dz], NORM_Z + 4 * dc + dz)
        part = part + nz[dc, dz]
    sx[...] = part
    first_count, first_sent = count[0], list(sent)

    def gather(own):
        for dy, dx in plane:
            kind = (own + dy + dx) % 2
            put(sx.at[kind], npl.at[4 * dy + dx], at(0, dy, dx, 0), NORM_P + 4 * dy + dx)
        npl[0] = part[own]
        order = sorted(plane, key=lambda off: -((off[0] == 2) + (off[1] == 2) + (off[0] > 0) + (off[1] > 0)))
        for kind, gat, slot in ((0, gat1, DATA_Z1), (1, gat2, DATA_Z2)):
            for k in range(1, RING):
                arrived(gat.at[0, k], slot + k)
            for dy, dx in order:
                if (own + dy + dx) % 2 == kind:
                    put(gat.at[0], gat.at[4 * dy + dx], at(0, dy, dx, 0), DATA_P + 4 * dy + dx)

    def inverse_norm():
        total = npl[0]
        for dy, dx in plane:
            arrived(npl.at[4 * dy + dx], NORM_P + 4 * dy + dx)
            total = total + npl[4 * dy + dx]
        return 1.0 / (jnp.sqrt(jnp.sum(total, keepdims=True)) + NORM_EPS)

    def hand_out(src, dst, slot):
        keep = pltpu.make_async_copy(src.at[0, 0], dst.at[z], recv_sem.at[slot + z])
        keep.start()
        for dx in range(2):
            for dz in range(RING):
                if (dx, dz) != (0, 0):
                    put(src.at[dx, dz], dst.at[z], at(dz, 0, dx, 0), slot + z)

    own_cols, other_cols = pl.ds(0, ROWS), pl.ds(ROWS, ROWS)
    parity = lax.rem(x + y, 2)

    @pl.when(parity == 0)
    def fc1():
        gather(0)
        inv = inverse_norm()
        arrive = []
        for c in range(4):
            for s in range(4 * c, 4 * c + 4):
                if s:
                    arrived(gat1.at[s], DATA_P + s)
            rows = pl.ds(256 * c, 256)
            ya[rows, own_cols] = (gat1[4 * c:4 * c + 4].reshape(256, ROWS).astype(F32) * inv).astype(BF16)
            arrive.append(trade(ya.at[rows, own_cols], ya.at[rows, other_cols]))
        for step in range(NS_STEPS):
            cur, nxt = (ya, yb) if step % 2 == 0 else (yb, ya)
            gram, panel = (aa, ra) if step % 2 == 0 else (ab, rb)
            gram[0:ROWS, :] = dot(cur[:, 0:ROWS], cur[:, 0:ROWS], 0, 0).astype(BF16)
            swap = trade(gram.at[pl.ds(0, ROWS)], panel.at[:, other_cols])
            half[...] = dot(gram[0:ROWS, :], gram[0:ROWS, :], 1, 0)
            for copy in arrive:
                copy.wait_recv()
            cross = dot(cur[:, ROWS:], cur[:, 0:ROWS], 0, 0).astype(BF16)
            gram[ROWS:, :] = cross
            panel[:, 0:ROWS] = cross
            square = half[...] + dot(gram[ROWS:, :], gram[ROWS:, :], 0, 0)
            b1[0:ROWS, :] = (NS_COEF_B * gram[0:ROWS, :].astype(F32) + NS_COEF_C * square).astype(BF16)
            swap.wait_recv()
            square = dot(panel[...], gram[...], 1, 0)
            b1[ROWS:, :] = (NS_COEF_B * gram[ROWS:, :].astype(F32) + NS_COEF_C * square).astype(BF16)
            flush()
            if step < NS_STEPS - 1:
                arrive = []
                base = 0
                for size in CHUNKS:
                    rows = pl.ds(base, size)
                    upd = NS_COEF_A * cur[rows, 0:ROWS].astype(F32) + dot(cur[rows, :], b1[...], 1, 0)
                    nxt[rows, 0:ROWS] = upd.astype(BF16)
                    arrive.append(trade(nxt.at[rows, own_cols], nxt.at[rows, other_cols]))
                    base += size
            else:
                upd = NS_COEF_A * cur[0:128, 0:ROWS].astype(F32) + dot(cur[0:128, :], b1[...], 1, 0)
                xo1[...] = upd.astype(BF16).reshape(2, RING, C1, ROWS)
                hand_out(xo1, o1, OUT1)
        flush()

    count[0] = first_count
    swaps[0] = 0
    sent[:] = first_sent

    @pl.when(parity == 1)
    def fc2():
        gather(1)
        inv = inverse_norm()
        for s in range(1, 16):
            arrived(gat2.at[s], DATA_P + s)
        y2a[:, 0:ROWS] = (gat2[...].reshape(N2, ROWS).astype(F32) * inv).astype(BF16)
        arrive = trade(y2a.at[:, own_cols], y2a.at[:, other_cols])
        for step in range(NS_STEPS):
            cur, nxt = (y2a, y2b) if step % 2 == 0 else (y2b, y2a)
            arrive.wait_recv()
            a2[...] = dot(cur[...], cur[...], 1, 1).astype(BF16)
            b2[...] = (NS_COEF_B * a2[...].astype(F32) + NS_COEF_C * dot(a2[...], a2[...], 1, 0)).astype(BF16)
            flush()
            if step < NS_STEPS - 1:
                upd = NS_COEF_A * cur[:, 0:ROWS].astype(F32) + dot(b2[...], cur[:, 0:ROWS], 1, 0)
                nxt[:, 0:ROWS] = upd.astype(BF16)
                arrive = trade(nxt.at[:, own_cols], nxt.at[:, other_cols])
            else:
                upd = NS_COEF_A * cur[0:64, 0:ROWS].astype(F32) + dot(b2[0:64, :], cur[:, 0:ROWS], 1, 0)
                xo2[...] = upd.astype(BF16).reshape(2, RING, C2, ROWS)
                hand_out(xo2, o2, OUT2)
        flush()

    for e in range(EXPERTS):
        arrived(o2.at[e], OUT2 + e)
        arrived(o1.at[e], OUT1 + e)


def muon(m1, g1, m2, g2):
    vmem = pl.BlockSpec(memory_space=pltpu.VMEM)
    hbm = pl.BlockSpec(memory_space=pltpu.HBM)
    big, small = (EXPERTS, C1, ROWS), (EXPERTS, C2, ROWS)
    scratch = [
        pltpu.VMEM(big, F32), pltpu.VMEM(big, BF16), pltpu.VMEM(small, F32), pltpu.VMEM(small, BF16),
        pltpu.VMEM(big, BF16), pltpu.VMEM(small, BF16),
        pltpu.VMEM((EXPERTS, 2, 8, 128), F32), pltpu.VMEM((2, RING, 2, 8, 128), F32),
        pltpu.VMEM((16, 8, 128), F32), pltpu.VMEM((2, 8, 128), F32),
        pltpu.VMEM((16, RING, C1, ROWS), BF16), pltpu.VMEM((16, RING, C2, ROWS), BF16),
        pltpu.VMEM((N1, 2 * ROWS), BF16), pltpu.VMEM((N1, 2 * ROWS), BF16),
        pltpu.VMEM((2 * ROWS, ROWS), BF16), pltpu.VMEM((2 * ROWS, ROWS), BF16),
        pltpu.VMEM((ROWS, 2 * ROWS), BF16), pltpu.VMEM((ROWS, 2 * ROWS), BF16),
        pltpu.VMEM((2 * ROWS, ROWS), BF16), pltpu.VMEM((ROWS, ROWS), F32),
        pltpu.VMEM((N2, 2 * ROWS), BF16), pltpu.VMEM((N2, 2 * ROWS), BF16),
        pltpu.VMEM((N2, N2), BF16), pltpu.VMEM((N2, N2), BF16),
        pltpu.VMEM((2, RING, C1, ROWS), BF16), pltpu.VMEM((2, RING, C2, ROWS), BF16),
        pltpu.SemaphoreType.DMA((4,)), pltpu.SemaphoreType.DMA((SEMS,)), pltpu.SemaphoreType.DMA((SEMS,)),
    ]
    return pl.pallas_call(
        kernel, name='muon',
        out_shape=[jax.ShapeDtypeStruct(big, BF16), jax.ShapeDtypeStruct(small, BF16)],
        in_specs=[hbm] * 4, out_specs=[vmem] * 2, scratch_shapes=scratch,
        cost_estimate=pl.CostEstimate(flops=16_000_000_000, bytes_accessed=1 << 20, transcendentals=0),
        compiler_params=pltpu.CompilerParams(
            collective_id=0, has_side_effects=True, vmem_limit_bytes=63 << 20),
    )(m1, g1, m2, g2)


def solution(mesh):
    block_spec = P('stage', 'data', 'model')

    def local_step(w_fc1, m_fc1, g_fc1, w_fc2, m_fc2, g_fc2):
        turn = lambda arr: jnp.transpose(arr, (0, 2, 1))
        o_fc1, o_fc2 = muon(turn(m_fc1), turn(g_fc1), turn(m_fc2), turn(g_fc2))
        outs = []
        for w, m, g, o in ((w_fc1, m_fc1, g_fc1, o_fc1), (w_fc2, m_fc2, g_fc2, o_fc2)):
            step = turn(o).astype(F32) * STEP_SCALE
            outs += [w - LEARN_RATE * (step + DECAY * w), MOMENTUM * m + g.astype(F32)]
        return tuple(outs)

    return jax.shard_map(local_step, mesh=mesh, in_specs=(block_spec,) * 6, out_specs=(block_spec,) * 4, check_vma=False)
```

profile of v0, /device:TPU:1, one launch (start us, length us, event | category | flops | bytes accessed | tf_op | source)
XLA Modules:
  0.0 58.9 jit_solution(10878851926259966763)
XLA Ops:
  0.6 0.0 copy-start
  0.6 0.0 copy-start.1
  0.7 0.0 copy-start.2
  0.7 55.8 %muon.1 = (bf16[4,16,512]{2,1,0:T(8,128)(2,1)}, bf16[4,8,512]{2,1,0:T(8,128)(2,1)}) custom-call(f32[4,16,512]{2,1,0:T(8,128)} %bitcast.16, bf16[4,16,512]{2,1,0:T(8,128)(2,1)} %bitcast.17, f32[4,8,512]{2,1,0:T(8,128)} %bitcast.18, bf16[4,8,512]{2,1,0:T(8,128)(2,1)} %bitcast.19), custom_call_target="tpu_custom_call" | custom-call | flops 16000000000 | bytes 1048576 | tf_op jit(solution)/shard_map/muon/pallas_call | solution.py:259
  56.5 0.0 copy-done
  56.5 0.0 copy-done.1
  56.5 0.0 copy-done.2
  56.5 0.0 copy-start.3
  56.5 0.0 copy-start.4
  56.5 0.0 copy-start.5
  56.5 0.0 copy-start.6
  56.6 1.6 %fusion.1 = (f32[4,512,16]{1,2,0:T(8,128)}, f32[4,512,16]{1,2,0:T(8,128)}) fusion(f32[4,512,16]{1,2,0:T(8,128)S(1)} %copy-done, bf16[4,16,512]{2,1,0:T(8,128)(2,1)} %get-tuple-element.6, bf16[4,512,16]{1,2,0:T(8,128)(2,1)S(1)} %copy-done.2, f32[4,512,16]{1,2,0:T(8,128)S(1)} %copy-done.1), kind=kLoop, calls=%fused_computation.2 | loop fusion | flops 294912 | bytes 655360 | tf_op jit(solution)/shard_map/sub | solution.py:278
  58.2 0.0 copy-done.3
  58.2 0.0 copy-done.4
  58.2 0.0 copy-done.5
  58.2 0.0 copy-done.6
  58.2 0.7 %fusion.3 = (f32[4,512,8]{1,2,0:T(8,128)}, f32[4,512,8]{1,2,0:T(8,128)}) fusion(f32[4,512,8]{1,2,0:T(8,128)S(1)} %copy-done.4, bf16[4,8,512]{2,1,0:T(8,128)(2,1)S(1)} %copy-done.6, bf16[4,512,8]{1,2,0:T(8,128)(2,1)S(1)} %copy-done.5, f32[4,512,8]{1,2,0:T(8,128)S(1)} %copy-done.3), kind=kLoop, calls=%fused_computation.6 | loop fusion | flops 147456 | bytes 327680 | tf_op jit(solution)/shard_map/sub | solution.py:278
Async XLA Ops:
  0.6 55.8 %copy-start = (f32[4,512,16]{1,2,0:T(8,128)S(1)}, f32[4,512,16]{1,2,0:T(8,128)}, u32[]{:S(2)}) copy-start(f32[4,512,16]{1,2,0:T(8,128)} %param.6) | copy-start | bytes 393220
  0.6 55.8 %copy-start.1 = (f32[4,512,16]{1,2,0:T(8,128)S(1)}, f32[4,512,16]{1,2,0:T(8,128)}, u32[]{:S(2)}) copy-start(f32[4,512,16]{1,2,0:T(8,128)} %param.7) | copy-start | bytes 393220
  0.7 55.8 %copy-start.2 = (bf16[4,512,16]{1,2,0:T(8,128)(2,1)S(1)}, bf16[4,512,16]{1,2,0:T(8,128)(2,1)}, u32[]{:S(2)}) copy-start(bf16[4,512,16]{1,2,0:T(8,128)(2,1)} %param.8) | copy-start | bytes 196612
  56.5 1.7 %copy-start.3 = (f32[4,512,8]{1,2,0:T(8,128)S(1)}, f32[4,512,8]{1,2,0:T(8,128)}, u32[]{:S(2)}) copy-start(f32[4,512,8]{1,2,0:T(8,128)} %param.10) | copy-start | bytes 196612
  56.5 1.7 %copy-start.4 = (f32[4,512,8]{1,2,0:T(8,128)S(1)}, f32[4,512,8]{1,2,0:T(8,128)}, u32[]{:S(2)}) copy-start(f32[4,512,8]{1,2,0:T(8,128)} %param.9) | copy-start | bytes 196612
  56.5 1.7 %copy-start.5 = (bf16[4,512,8]{1,2,0:T(8,128)(2,1)S(1)}, bf16[4,512,8]{1,2,0:T(8,128)(2,1)}, u32[]{:S(2)}) copy-start(bf16[4,512,8]{1,2,0:T(8,128)(2,1)} %param.11) | copy-start | bytes 98308
  56.5 1.7 %copy-start.6 = (bf16[4,8,512]{2,1,0:T(8,128)(2,1)S(1)}, bf16[4,8,512]{2,1,0:T(8,128)(2,1)}, u32[]{:S(2)}) copy-start(bf16[4,8,512]{2,1,0:T(8,128)(2,1)} %get-tuple-element.7) | copy-start | bytes 98308
where the time goes:
time: 59.1 us; the launch traced here: 58.9 us
  Pallas kernels  55.8 us (94%)
  other arithmetic  2.3 us (4%)
  between operations  0.73 us (1%)
    pallas_call x1, Pallas kernels, muon(): pl.pallas_call(kernel, name='muon', out_shape=[jax.ShapeDtypeStruct(big,...  55.8 us
    sub x2, other arithmetic, local_step(): outs += [w - LEARN_RATE * (step + DECAY * w), MOMENTUM * m + g.astype(F32)]  2.3 us

commit v1 on v0

--- a/solution.py
+++ b/solution.py
@@ -22,7 +22,8 @@
 C1, C2 = 16, 8
 N1, N2 = 1024, 512
 STEP_SCALE = 0.2 * math.sqrt(1024)
-CHUNKS = (256, 256, 256, 256)
+CHUNKS = (384, 384, 256)
+ARRIVAL = (0, 1, 3, 2)
 NORM_Z, DATA_Z1, DATA_Z2, NORM_P, DATA_P, OUT1, OUT2, SWAP = 0, 8, 12, 16, 32, 48, 52, 56
 SEMS = 160
 
@@ -51,8 +52,8 @@
 
 
 def kernel(m1h, g1h, m2h, g2h, o1, o2,
-           m1, g1, m2, g2, mb1, mb2, nb, nz, npl, sx, gat1, gat2,
-           ya, yb, aa, ab, ra, rb, b1, half, y2a, y2b, a2, b2, xo1, xo2, load_sem, send_sem, recv_sem):
+           m1, g1, m2, g2, mb1, mb2, nb, nz, npl, sx, total, gat1, gat2,
+           ya, yb, aa, ab, ra, rb, b1, half, acc, y2a, y2b, a2, b2, xo1, xo2, load_sem, send_sem, recv_sem):
     idx = lax.axis_index('model')
     core = lax.axis_index('data')
     z = lax.div(idx, 16)
@@ -105,55 +106,58 @@
         copy.start()
     for copy in loads:
         copy.wait()
+    nb[...] = jnp.zeros_like(nb)
     for e in range(EXPERTS):
         mom = MOMENTUM * m1[e] + g1[e].astype(F32)
         mb1[e] = mom.astype(BF16)
-        nb[e, 0] = fold(mom * mom)
+        nb[0, e:e + 1] = jnp.sum(fold(mom * mom), axis=0, keepdims=True)
         mom = MOMENTUM * m2[e] + g2[e].astype(F32)
         mb2[e] = mom.astype(BF16)
-        nb[e, 1] = fold(mom * mom)
+        nb[1, e:e + 1] = jnp.sum(fold(mom * mom), axis=0, keepdims=True)
+    gat1[0, 0] = mb1[z]
+    gat2[0, 0] = mb2[z]
     pl.semaphore_wait(barrier, len(greet))
 
-    for dz, dc in z_peers:
-        put(nb.at[flip(z, dz)], nz.at[dc, dz], at(dz, 0, 0, dc), NORM_Z + 4 * dc + dz)
-    for k in range(1, RING):
+    for k in (2, 1, 3):
         put(mb1.at[flip(z, k)], gat1.at[0, k], at(k, 0, 0, 0), DATA_Z1 + k)
     for k in range(1, RING):
         put(mb2.at[flip(z, k)], gat2.at[0, k], at(k, 0, 0, 0), DATA_Z2 + k)
-    gat1[0, 0] = mb1[z]
-    gat2[0, 0] = mb2[z]
-    part = nb[z]
-    for dz, dc in z_peers:
-        arrived(nz.at[dc, dz], NORM_Z + 4 * dc + dz)
-        part = part + nz[dc, dz]
-    sx[...] = part
     first_count, first_sent = count[0], list(sent)
 
     def gather(own):
-        for dy, dx in plane:
+        order = sorted(plane, key=lambda off: -((off[0] == 2) + (off[1] == 2) + (off[0] > 0) + (off[1] > 0)))
+        for dy, dx in order:
             kind = (own + dy + dx) % 2
-            put(sx.at[kind], npl.at[4 * dy + dx], at(0, dy, dx, 0), NORM_P + 4 * dy + dx)
-        npl[0] = part[own]
-        order = sorted(plane, key=lambda off: -((off[0] == 2) + (off[1] == 2) + (off[0] > 0) + (off[1] > 0)))
-        for kind, gat, slot in ((0, gat1, DATA_Z1), (1, gat2, DATA_Z2)):
-            for k in range(1, RING):
-                arrived(gat.at[0, k], slot + k)
+            put(nb.at[kind], npl.at[4 * dy + dx], at(0, dy, dx, 0), NORM_P + 4 * dy + dx)
+        for k in (0, 1, 3, 2):
+            if k:
+                arrived(gat1.at[0, k], DATA_Z1 + k)
             for dy, dx in order:
-                if (own + dy + dx) % 2 == kind:
-                    put(gat.at[0], gat.at[4 * dy + dx], at(0, dy, dx, 0), DATA_P + 4 * dy + dx)
-
-    def inverse_norm():
-        total = npl[0]
+                if (own + dy + dx) % 2 == 0:
+                    put(gat1.at[0, k], gat1.at[4 * dy + dx, k], at(0, dy, dx, 0), DATA_P + 4 * dy + dx)
+        part = nb[own]
         for dy, dx in plane:
             arrived(npl.at[4 * dy + dx], NORM_P + 4 * dy + dx)
-            total = total + npl[4 * dy + dx]
-        return 1.0 / (jnp.sqrt(jnp.sum(total, keepdims=True)) + NORM_EPS)
+            part = part + npl[4 * dy + dx]
+        sx[...] = part
+        for dz, dc in z_peers:
+            put(sx, nz.at[4 * dc + dz], at(dz, 0, 0, dc), NORM_Z + 4 * dc + dz)
+        for k in range(1, RING):
+            arrived(gat2.at[0, k], DATA_Z2 + k)
+        for dy, dx in order:
+            if (own + dy + dx) % 2 == 1:
+                put(gat2.at[0], gat2.at[4 * dy + dx], at(0, dy, dx, 0), DATA_P + 4 * dy + dx)
+        for dz, dc in z_peers:
+            arrived(nz.at[4 * dc + dz], NORM_Z + 4 * dc + dz)
+            part = part + nz[4 * dc + dz]
+        total[...] = part
+        return 1.0 / (jnp.sqrt(jnp.sum(total[pl.ds(z, 1), :], keepdims=True)) + NORM_EPS)
 
     def hand_out(src, dst, slot):
         keep = pltpu.make_async_copy(src.at[0, 0], dst.at[z], recv_sem.at[slot + z])
         keep.start()
-        for dx in range(2):
-            for dz in range(RING):
+        for dx in (1, 0):
+            for dz in (2, 1, 3, 0):
                 if (dx, dz) != (0, 0):
                     put(src.at[dx, dz], dst.at[z], at(dz, 0, dx, 0), slot + z)
 
@@ -162,33 +166,45 @@
 
     @pl.when(parity == 0)
     def fc1():
-        gather(0)
-        inv = inverse_norm()
+        inv = gather(0)
         arrive = []
-        for c in range(4):
+        for i, c in enumerate(ARRIVAL):
             for s in range(4 * c, 4 * c + 4):
                 if s:
                     arrived(gat1.at[s], DATA_P + s)
             rows = pl.ds(256 * c, 256)
             ya[rows, own_cols] = (gat1[4 * c:4 * c + 4].reshape(256, ROWS).astype(F32) * inv).astype(BF16)
             arrive.append(trade(ya.at[rows, own_cols], ya.at[rows, other_cols]))
+            piece = dot(ya[rows, 0:ROWS], ya[rows, 0:ROWS], 0, 0)
+            half[...] = piece if i == 0 else half[...] + piece
+            if i:
+                rows = pl.ds(256 * ARRIVAL[i - 1], 256)
+                arrive[i - 1].wait_recv()
+                piece = dot(ya[rows, ROWS:], ya[rows, 0:ROWS], 0, 0)
+                acc[...] = piece if i == 1 else acc[...] + piece
+        arrive = arrive[-1:]
         for step in range(NS_STEPS):
             cur, nxt = (ya, yb) if step % 2 == 0 else (yb, ya)
-            gram, panel = (aa, ra) if step % 2 == 0 else (ab, rb)
-            gram[0:ROWS, :] = dot(cur[:, 0:ROWS], cur[:, 0:ROWS], 0, 0).astype(BF16)
-            swap = trade(gram.at[pl.ds(0, ROWS)], panel.at[:, other_cols])
+            gram, far = (aa, ra) if step % 2 == 0 else (ab, rb)
+            near = half[...] if step == 0 else dot(cur[:, 0:ROWS], cur[:, 0:ROWS], 0, 0)
+            gram[0:ROWS, :] = near.astype(BF16)
+            swap = trade(gram.at[pl.ds(0, ROWS)], far)
             half[...] = dot(gram[0:ROWS, :], gram[0:ROWS, :], 1, 0)
             for copy in arrive:
                 copy.wait_recv()
-            cross = dot(cur[:, ROWS:], cur[:, 0:ROWS], 0, 0).astype(BF16)
-            gram[ROWS:, :] = cross
-            panel[:, 0:ROWS] = cross
+            if step == 0:
+                rows = pl.ds(256 * ARRIVAL[-1], 256)
+                cross = acc[...] + dot(cur[rows, ROWS:], cur[rows, 0:ROWS], 0, 0)
+            else:
+                cross = dot(cur[:, ROWS:], cur[:, 0:ROWS], 0, 0)
+            gram[ROWS:, :] = cross.astype(BF16)
             square = half[...] + dot(gram[ROWS:, :], gram[ROWS:, :], 0, 0)
             b1[0:ROWS, :] = (NS_COEF_B * gram[0:ROWS, :].astype(F32) + NS_COEF_C * square).astype(BF16)
+            acc[...] = dot(gram[ROWS:, :], gram[0:ROWS, :], 1, 0)
             swap.wait_recv()
-            square = dot(panel[...], gram[...], 1, 0)
+            flush()
+            square = acc[...] + dot(far[...], gram[ROWS:, :], 1, 0)
             b1[ROWS:, :] = (NS_COEF_B * gram[ROWS:, :].astype(F32) + NS_COEF_C * square).astype(BF16)
-            flush()
             if step < NS_STEPS - 1:
                 arrive = []
                 base = 0
@@ -210,8 +226,7 @@
 
     @pl.when(parity == 1)
     def fc2():
-        gather(1)
-        inv = inverse_norm()
+        inv = gather(1)
         for s in range(1, 16):
             arrived(gat2.at[s], DATA_P + s)
         y2a[:, 0:ROWS] = (gat2[...].reshape(N2, ROWS).astype(F32) * inv).astype(BF16)
@@ -244,13 +259,13 @@
     scratch = [
         pltpu.VMEM(big, F32), pltpu.VMEM(big, BF16), pltpu.VMEM(small, F32), pltpu.VMEM(small, BF16),
         pltpu.VMEM(big, BF16), pltpu.VMEM(small, BF16),
-        pltpu.VMEM((EXPERTS, 2, 8, 128), F32), pltpu.VMEM((2, RING, 2, 8, 128), F32),
-        pltpu.VMEM((16, 8, 128), F32), pltpu.VMEM((2, 8, 128), F32),
+        pltpu.VMEM((2, 8, 128), F32), pltpu.VMEM((2 * RING, 8, 128), F32), pltpu.VMEM((16, 8, 128), F32),
+        pltpu.VMEM((8, 128), F32), pltpu.VMEM((8, 128), F32),
         pltpu.VMEM((16, RING, C1, ROWS), BF16), pltpu.VMEM((16, RING, C2, ROWS), BF16),
         pltpu.VMEM((N1, 2 * ROWS), BF16), pltpu.VMEM((N1, 2 * ROWS), BF16),
         pltpu.VMEM((2 * ROWS, ROWS), BF16), pltpu.VMEM((2 * ROWS, ROWS), BF16),
-        pltpu.VMEM((ROWS, 2 * ROWS), BF16), pltpu.VMEM((ROWS, 2 * ROWS), BF16),
-        pltpu.VMEM((2 * ROWS, ROWS), BF16), pltpu.VMEM((ROWS, ROWS), F32),
+        pltpu.VMEM((ROWS, ROWS), BF16), pltpu.VMEM((ROWS, ROWS), BF16),
+        pltpu.VMEM((2 * ROWS, ROWS), BF16), pltpu.VMEM((ROWS, ROWS), F32), pltpu.VMEM((ROWS, ROWS), F32),
         pltpu.VMEM((N2, 2 * ROWS), BF16), pltpu.VMEM((N2, 2 * ROWS), BF16),
         pltpu.VMEM((N2, N2), BF16), pltpu.VMEM((N2, N2), BF16),
         pltpu.VMEM((2, RING, C1, ROWS), BF16), pltpu.VMEM((2, RING, C2, ROWS), BF16),
@@ -262,8 +277,8 @@
         in_specs=[hbm] * 4, out_specs=[vmem] * 2, scratch_shapes=scratch,
         cost_estimate=pl.CostEstimate(flops=16_000_000_000, bytes_accessed=1 << 20, transcendentals=0),
         compiler_params=pltpu.CompilerParams(
-            collective_id=0, has_side_effects=True, vmem_limit_bytes=63 << 20),
-    )(m1, g1, m2, g2)
+            collective_id=0, has_side_effects=True, vmem_limit_bytes=40 << 20),
+    )(*[pltpu.with_memory_space_constraint(arg, pltpu.HBM) for arg in (m1, g1, m2, g2)])
 
 
 def solution(mesh):

time: 59.1 us -> 52.5 us (0.89)
  Pallas kernels: 55.8 us -> 50.1 us
  other arithmetic: 2.3 us -> 1.42 us
    pallas_call x1, Pallas kernels: 55.8 us -> 50.1 us  [muon(): pl.pallas_call(kernel, name='muon', out_shape=[jax.ShapeDtypeStruct(big,...]
    sub x2, other arithmetic: 2.3 us -> 1.42 us  [local_step(): outs += [w - LEARN_RATE * (step + DECAY * w), MOMENTUM * m + g.astype(F32)]]
where the time goes in v1:
time: 52.5 us; the launch traced here: 52.4 us
  Pallas kernels  50.1 us (95%)
  other arithmetic  1.42 us (3%)
  between operations  0.71 us (1%)
    pallas_call x1, Pallas kernels, muon(): pl.pallas_call(kernel, name='muon', out_shape=[jax.ShapeDtypeStruct(big,...  50.1 us
    sub x2, other arithmetic, local_step(): outs += [w - LEARN_RATE * (step + DECAY * w), MOMENTUM * m + g.astype(F32)]  1.42 us

profile of v1, /device:TPU:1, one launch (start us, length us, event | category | flops | bytes accessed | tf_op | source)
XLA Modules:
  0.0 52.4 jit_solution(14106105456221835328)
XLA Ops:
  0.6 0.0 copy-start
  0.6 0.0 copy-start.1
  0.7 0.0 copy-start.2
  0.7 50.1 %muon.1 = (bf16[4,16,512]{2,1,0:T(8,128)(2,1)S(1)}, bf16[4,8,512]{2,1,0:T(8,128)(2,1)S(1)}) custom-call(f32[4,16,512]{2,1,0:T(8,128)} %bitcast.16, bf16[4,16,512]{2,1,0:T(8,128)(2,1)} %bitcast.17, f32[4,8,512]{2,1,0:T(8,128)} %bitcast.18, bf16[4,8,512]{2,1,0:T(8,128)(2,1)} %bitcast.19), custom_call_target="tpu_custom_call" | custom-call | flops 16000000000 | bytes 1048576 | tf_op jit(solution)/shard_map/muon/pallas_call | solution.py:274
  50.8 0.0 copy-done
  50.8 0.0 copy-done.1
  50.8 0.0 copy-done.2
  50.8 0.0 copy-start.3
  50.8 0.0 copy-start.4
  50.8 0.0 copy-start.5
  50.8 0.7 %fusion.1 = (f32[4,512,16]{1,2,0:T(8,128)}, f32[4,512,16]{1,2,0:T(8,128)}) fusion(f32[4,512,16]{1,2,0:T(8,128)S(1)} %copy-done, bf16[4,16,512]{2,1,0:T(8,128)(2,1)S(1)} %get-tuple-element.6, bf16[4,512,16]{1,2,0:T(8,128)(2,1)S(1)} %copy-done.2, f32[4,512,16]{1,2,0:T(8,128)S(1)} %copy-done.1), kind=kLoop, calls=%fused_computation.2 | loop fusion | flops 294912 | bytes 655360 | tf_op jit(solution)/shard_map/sub | solution.py:293
  51.6 0.1 copy-done.3
  51.6 0.0 copy-done.4
  51.7 0.0 copy-done.5
  51.7 0.7 %fusion.3 = (f32[4,512,8]{1,2,0:T(8,128)}, f32[4,512,8]{1,2,0:T(8,128)}) fusion(f32[4,512,8]{1,2,0:T(8,128)S(1)} %copy-done.4, bf16[4,8,512]{2,1,0:T(8,128)(2,1)S(1)} %get-tuple-element.7, bf16[4,512,8]{1,2,0:T(8,128)(2,1)S(1)} %copy-done.5, f32[4,512,8]{1,2,0:T(8,128)S(1)} %copy-done.3), kind=kLoop, calls=%fused_computation.6 | loop fusion | flops 147456 | bytes 327680 | tf_op jit(solution)/shard_map/sub | solution.py:293
Async XLA Ops:
  0.6 50.1 %copy-start = (f32[4,512,16]{1,2,0:T(8,128)S(1)}, f32[4,512,16]{1,2,0:T(8,128)}, u32[]{:S(2)}) copy-start(f32[4,512,16]{1,2,0:T(8,128)} %param.6) | copy-start | bytes 393220
  0.6 50.1 %copy-start.1 = (f32[4,512,16]{1,2,0:T(8,128)S(1)}, f32[4,512,16]{1,2,0:T(8,128)}, u32[]{:S(2)}) copy-start(f32[4,512,16]{1,2,0:T(8,128)} %param.7) | copy-start | bytes 393220
  0.7 50.1 %copy-start.2 = (bf16[4,512,16]{1,2,0:T(8,128)(2,1)S(1)}, bf16[4,512,16]{1,2,0:T(8,128)(2,1)}, u32[]{:S(2)}) copy-start(bf16[4,512,16]{1,2,0:T(8,128)(2,1)} %param.8) | copy-start | bytes 196612
  50.8 0.8 %copy-start.3 = (f32[4,512,8]{1,2,0:T(8,128)S(1)}, f32[4,512,8]{1,2,0:T(8,128)}, u32[]{:S(2)}) copy-start(f32[4,512,8]{1,2,0:T(8,128)} %param.10) | copy-start | bytes 196612
  50.8 0.9 %copy-start.4 = (f32[4,512,8]{1,2,0:T(8,128)S(1)}, f32[4,512,8]{1,2,0:T(8,128)}, u32[]{:S(2)}) copy-start(f32[4,512,8]{1,2,0:T(8,128)} %param.9) | copy-start | bytes 196612
  50.8 0.9 %copy-start.5 = (bf16[4,512,8]{1,2,0:T(8,128)(2,1)S(1)}, bf16[4,512,8]{1,2,0:T(8,128)(2,1)}, u32[]{:S(2)}) copy-start(bf16[4,512,8]{1,2,0:T(8,128)(2,1)} %param.11) | copy-start | bytes 98308
